TPU v7x, 32 devices: a whole 2x2x4 slice. The times are simulated.
32 devices in a mesh: prow: 8 (over z, y), pcol: 4 (over x, core).
Axes of the slice: x: 2, y: 2, z: 4, core: 2. Of those that a mesh axis runs over, the one named last changes fastest.
Arguments:
- inverse_block: bfloat16 [2, 512, 512], P(None, 'prow', 'pcol'), may hold values from -1.75 to 1.75
- panel: bfloat16 [2, 512, 2048], P(None, ('prow', 'pcol')), may hold values from -0.5 to 0.5
- pattern: int32 [1, 4], replicated, may hold values 0 or 1
- diag_inverse: float32 [2, 512, 2048], P(None, None, 'pcol'), may hold values from -6 to 6
Outputs:
- offdiag: bfloat16 [2, 512, 2048], P(None, 'prow', 'pcol')
- diagonal: float32 [2, 512, 2048], P(None, None, 'pcol')
All inputs are finite; a program needn't handle non-finite values.
Results may differ from a plain program's by a relative error of at most 0.0024.
Values may be sent and summed in bfloat16 or wider, within the bound.
A program may use at most 64 MiB of HBM per device.

v0:
```python
import jax
import jax.numpy as jnp
from jax import lax
from jax.sharding import PartitionSpec as P

WIDTH = 512


def complex_product(left_real, left_imag, right_real, right_imag, contract):
    dims = (((contract,), (0,)), ((), ()))
    real_part = lax.dot_general(
        left_real, right_real, dims, preferred_element_type=jnp.float32
    ) - lax.dot_general(left_imag, right_imag, dims, preferred_element_type=jnp.float32)
    imag_part = lax.dot_general(
        left_real, right_imag, dims, preferred_element_type=jnp.float32
    ) + lax.dot_general(left_imag, right_real, dims, preferred_element_type=jnp.float32)
    return (real_part, imag_part)


def keep_table(pattern, row_start, row_count, col_start, col_count, block_width):
    row_ids = (row_start + jnp.arange(row_count, dtype=jnp.int32)) // block_width
    col_ids = (col_start + jnp.arange(col_count, dtype=jnp.int32)) // block_width
    row_select = (
        row_ids[:, None] == jnp.arange(pattern.shape[0], dtype=jnp.int32)[None, :]
    ).astype(jnp.float32)
    col_select = (
        col_ids[:, None] == jnp.arange(pattern.shape[1], dtype=jnp.int32)[None, :]
    ).astype(jnp.float32)
    pattern_value = pattern.astype(jnp.float32)
    row_pattern = jnp.dot(row_select, pattern_value, precision=lax.Precision.HIGHEST)
    return jnp.dot(row_pattern, col_select.T, precision=lax.Precision.HIGHEST)


def local(inverse_block, panel, pattern, diag_inverse):
    rows_dev = inverse_block.shape[1]
    block_span = inverse_block.shape[2]
    fine_rows = panel.shape[1]
    columns = panel.shape[2]
    row_index = lax.axis_index("prow")
    col_index = lax.axis_index("pcol")
    col_count = lax.axis_size("pcol")
    root_count = lax.axis_size("prow") // col_count
    fine_start = (row_index * col_count + col_index) * fine_rows
    keep_mask = keep_table(pattern, fine_start, fine_rows, 0, columns, WIDTH)
    masked = jnp.where(keep_mask[None] > 0.5, panel, jnp.zeros_like(panel))
    row_panel = lax.all_gather(masked, "pcol", axis=1, tiled=True)
    flipped = jnp.swapaxes(inverse_block, 1, 2)
    split_cols = flipped.reshape(2, root_count, col_count, fine_rows, rows_dev)
    received = lax.all_to_all(split_cols, "pcol", split_axis=2, concat_axis=1, tiled=True)
    regrouped = received.reshape(2, block_span, rows_dev)
    panel_piece = lax.all_gather(masked, "prow", axis=1, tiled=True)
    part_real, part_imag = complex_product(
        regrouped[0], regrouped[1], panel_piece[0], panel_piece[1], 0
    )
    stacked = jnp.stack([part_real, part_imag])
    summed = lax.psum_scatter(stacked, "pcol", scatter_dimension=2, tiled=True)
    local_cols = summed.shape[2]
    keep_local = keep_table(
        pattern, row_index * rows_dev, rows_dev, col_index * local_cols, local_cols, WIDTH
    )
    coupled = (summed * keep_local[None]).astype(jnp.bfloat16)
    offdiag = -coupled
    block_start = col_index * local_cols // WIDTH * WIDTH
    lower_panel = lax.dynamic_slice_in_dim(row_panel, block_start, WIDTH, 2)
    diag_real, diag_imag = complex_product(
        lower_panel[0], lower_panel[1], coupled[0], coupled[1], 0
    )
    shares = lax.psum_scatter(
        jnp.stack([diag_real, diag_imag]), "prow", scatter_dimension=1, tiled=True
    )
    correction = lax.all_gather(shares, "prow", axis=1, tiled=True)
    return (offdiag, diag_inverse + correction)


def solution(mesh):
    in_specs = (
        P(None, "prow", "pcol"),
        P(None, ("prow", "pcol"), None),
        P(),
        P(None, None, "pcol"),
    )
    out_specs = (P(None, "prow", "pcol"), P(None, None, "pcol"))
    return jax.shard_map(local, mesh=mesh, in_specs=in_specs, out_specs=out_specs, check_vma=False)
```

profile of v0, /device:TPU:0, one launch (start us, length us, event | category | flops | bytes accessed | tf_op | source)
XLA Modules:
  0.0 214.8 jit_solution(16898340930722284187)
XLA Ops:
  7.2 0.7 convert_bitcast_fusion
  7.9 0.7 convolution_compare_fusion
  8.6 1.6 broadcast_select_fusion
  10.3 0.9 copy.9
  11.2 0.1 reshape.60
  11.3 8.0 %all_to_all.15 = bf16[4,2,2048]{2,1,0:T(2,128)(2,1)S(1)} all-to-all(bf16[4,2,2048]{2,1,0:T(2,128)(2,1)S(1)} %reshape.60), channel_id=1, replica_groups=mesh['prow'=8,'pcol'=4] {'pcol'}, dimensions={0} | all-to-all | bytes 65536 | tf_op jit(solution)/shard_map/all_to_all | solution.py:49
  19.4 34.3 %all-gather.3.cloned.1.call-done = bf16[2,128,2048]{2,1,0:T(8,128)(2,1)} async-done(((bf16[2,16,2048]{2,1,0:T(8,128)(2,1)}), bf16[2,128,2048]{2,1,0:T(8,128)(2,1)}) %all-gather.3.cloned.1.call-update) | async-done | bytes 1048592 | tf_op jit(solution)/shard_map/all_gather | solution.py:51
  53.7 1.4 fusion.6
  55.1 1.3 fusion.5
  56.5 0.3 fusion.1
  56.8 0.3 fusion
  57.0 1.0 pad_maximum_fusion.1
  58.2 7.2 %all_gather.10 = bf16[2,64,2048]{2,1,0:T(8,128)(2,1)S(1)} all-gather(bf16[2,16,2048]{2,1,0:T(8,128)(2,1)S(1)} %copy-done.2), channel_id=1, replica_groups=mesh['prow'=8,'pcol'=4] {'pcol'}, dimensions={1}, use_global_device_ids=true | all-gather | bytes 655360 | tf_op jit(solution)/shard_map/all_gather | solution.py:46
  65.4 0.4 fusion.7
  65.7 16.0 %reduce-scatter.3.cloned.1.call-done = f32[2,64,512]{2,1,0:T(8,128)} async-done(((f32[2,64,2048]{2,1,0:T(8,128)}), f32[2,64,512]{2,1,0:T(8,128)}) %reduce-scatter.3.cloned.1.call-update) | async-done | bytes 262160 | tf_op jit(solution)/shard_map/reduce_scatter | solution.py:56
  81.8 1.6 fusion.27
  83.4 0.3 fusion.9
  83.8 0.3 fusion.10
  84.1 0.3 fusion.3
  84.4 0.3 fusion.2
  84.7 1.5 pad_maximum_fusion
  86.3 68.4 %reduce-scatter.5.cloned.1.call-done = f32[2,64,512]{2,1,0:T(8,128)} async-done(((f32[2,512,512]{2,1,0:T(8,128)}), f32[2,64,512]{2,1,0:T(8,128)}) %reduce-scatter.5.cloned.1.call-update) | async-done | bytes 262160 | tf_op jit(solution)/shard_map/reduce_scatter | solution.py:68
  154.8 50.1 %all-gather.5.cloned.1.call-done = f32[2,512,512]{2,1,0:T(8,128)} async-done(((f32[2,64,512]{2,1,0:T(8,128)}), f32[2,512,512]{2,1,0:T(8,128)}) %all-gather.5.cloned.1.call-update) | async-done | bytes 2097168 | tf_op jit(solution)/shard_map/all_gather | solution.py:71
  204.9 3.4 %add.76 = f32[2,512,512]{2,1,0:T(8,128)} add(f32[2,512,512]{2,1,0:T(8,128)S(1)} %copy-done.1, f32[2,512,512]{2,1,0:T(8,128)} %all-gather.5.cloned.1.call-done) | non-fusion elementwise | flops 524288 | bytes 6291456 | tf_op jit(solution)/shard_map/add | solution.py:72
  (22 shorter events, 0.4 us)
Async XLA Ops:
  7.2 46.6 %all-gather.3.cloned.1.call-start = ((), (), s32[]{:S(2)}) async-start(), calls=%async_computation.3 | async-start | bytes 1179648 | tf_op jit(solution)/shard_map/all_gather | solution.py:51
  10.2 71.5 %reduce-scatter.3.cloned.1.call-start = ((), (), s32[]{:S(2)}) async-start(), calls=%async_computation.4 | async-start | bytes 1310720 | tf_op jit(solution)/shard_map/reduce_scatter | solution.py:56
  53.7 2.7 %copy-start = (bf16[2,128,2048]{2,1,0:T(8,128)(2,1)S(1)}, bf16[2,128,2048]{2,1,0:T(8,128)(2,1)}, u32[]{:S(2)}) copy-start(bf16[2,128,2048]{2,1,0:T(8,128)(2,1)} %all-gather.3.cloned.1.call-done) | copy-start | bytes 3145732
  56.7 1.5 copy-start.2
  58.1 96.6 %reduce-scatter.5.cloned.1.call-start = ((), (), s32[]{:S(2)}) async-start(), calls=%async_computation.5 | async-start | bytes 2359296 | tf_op jit(solution)/shard_map/reduce_scatter | solution.py:68
  86.2 118.6 %copy-start.1 = (f32[2,512,512]{2,1,0:T(8,128)S(1)}, f32[2,512,512]{2,1,0:T(8,128)}, u32[]{:S(2)}) copy-start(f32[2,512,512]{2,1,0:T(8,128)} %param.7) | copy-start | bytes 6291460
  86.3 118.6 %all-gather.5.cloned.1.call-start = ((), (), s32[]{:S(2)}) async-start(), calls=%async_computation.6 | async-start | bytes 2359296 | tf_op jit(solution)/shard_map/all_gather | solution.py:71
Sparse Core Ops, SparseCore 0:
  10.7 42.9 all-gather.2
  58.2 23.5 reduce-scatter.2
  86.4 68.3 reduce-scatter.4
  156.8 48.0 all-gather.4
where the time goes:
time: 215 us
  waiting for transfers between devices  169 us (79%)
  blocking collectives  15.1 us (7%)
  between operations  13.9 us (6%)
  other arithmetic  9.83 us (5%)
  matrix products  5.66 us (3%)
    reduce_scatter x1, waiting for transfers between devices, local(): lax.psum_scatter(jnp.stack([diag_real, diag_imag]), 'prow', scatter_dimen...  68.4 us
    all_gather x1, waiting for transfers between devices, local(): correction = lax.all_gather(shares, 'prow', axis=1, tiled=True)  50.1 us
    all_gather x1, waiting for transfers between devices, local(): panel_piece = lax.all_gather(masked, 'prow', axis=1, tiled=True)  34.3 us
    reduce_scatter x1, waiting for transfers between devices, local(): summed = lax.psum_scatter(stacked, 'pcol', scatter_dimension=2, tiled=True)  16 us
    all_to_all x1, blocking collectives, local(): lax.all_to_all(split_cols, 'pcol', split_axis=2, concat_axis=1, tiled=True)  7.98 us
    all_gather x1, blocking collectives, local(): row_panel = lax.all_gather(masked, 'pcol', axis=1, tiled=True)  7.15 us
  transfers between devices with their start and end apart: 4, of which 4 were waited for; matrix products, arithmetic and copies ran while one was open for 1% of the time, Pallas kernels for 0%

commit v1 on v0

--- a/solution.py
+++ b/solution.py
@@ -48,7 +48,13 @@
     split_cols = flipped.reshape(2, root_count, col_count, fine_rows, rows_dev)
     received = lax.all_to_all(split_cols, "pcol", split_axis=2, concat_axis=1, tiled=True)
     regrouped = received.reshape(2, block_span, rows_dev)
-    panel_piece = lax.all_gather(masked, "prow", axis=1, tiled=True)
+    size = lax.axis_size("prow")
+    block, blocks = (masked, [masked])
+    for _ in range(size - 1):
+        block = lax.ppermute(block, "prow", [(i, (i + 1) % size) for i in range(size)])
+        blocks.insert(0, block)
+    line = jnp.concatenate(blocks, axis=1)
+    panel_piece = jnp.roll(line, (lax.axis_index("prow") + 1) * masked.shape[1], axis=1)
     part_real, part_imag = complex_product(
         regrouped[0], regrouped[1], panel_piece[0], panel_piece[1], 0
     )

time: 215 us -> 224 us (1.042)
  waiting for transfers between devices: 169 us -> 182 us
  blocking collectives: 15.1 us -> 6.5 us
  starting transfers between devices: 0.16 us -> 6.51 us
    ppermute x0 -> x7, waiting for transfers between devices: none -> 45.3 us  [local(): lax.ppermute(block, 'prow', [(i, (i + 1) % size) for i in range(size)])]
    all_gather x1 -> x0, waiting for transfers between devices: 34.3 us -> none  [local(): panel_piece = lax.all_gather(masked, 'prow', axis=1, tiled=True)]
    all_to_all x1 -> x0, blocking collectives: 7.98 us -> none  [local(): lax.all_to_all(split_cols, 'pcol', split_axis=2, concat_axis=1, tiled=True)]
    all_to_all x0 -> x1, waiting for transfers between devices: none -> 3.84 us  [local(): lax.all_to_all(split_cols, 'pcol', split_axis=2, concat_axis=1, tiled=True)]
    all_to_all x0 -> x1, starting transfers between devices: none -> 3.26 us  [local(): lax.all_to_all(split_cols, 'pcol', split_axis=2, concat_axis=1, tiled=True)]
    ppermute x0 -> x7, starting transfers between devices: none -> 3.12 us  [local(): lax.ppermute(block, 'prow', [(i, (i + 1) % size) for i in range(size)])]
  transfers between devices with their start and end apart: 4 -> 11, of which waited for: 4 -> 10; matrix products, arithmetic and copies ran while one was open for 1% -> 1% of each run, Pallas kernels for 0% -> 0%
where the time goes in v1:
time: 224 us
  waiting for transfers between devices  182 us (81%)
  between operations  14.1 us (6%)
  other arithmetic  9.27 us (4%)
  starting transfers between devices  6.51 us (3%)
  blocking collectives  6.5 us (3%)
  matrix products  3.51 us (2%)
    reduce_scatter x1, waiting for transfers between devices, local(): lax.psum_scatter(jnp.stack([diag_real, diag_imag]), 'prow', scatter_dimen...  68.7 us
    all_gather x1, waiting for transfers between devices, local(): correction = lax.all_gather(shares, 'prow', axis=1, tiled=True)  50.3 us
    ppermute x7, waiting for transfers between devices, local(): lax.ppermute(block, 'prow', [(i, (i + 1) % size) for i in range(size)])  45.3 us
    reduce_scatter x1, waiting for transfers between devices, local(): summed = lax.psum_scatter(stacked, 'pcol', scatter_dimension=2, tiled=True)  13.8 us
    all_gather x1, blocking collectives, local(): row_panel = lax.all_gather(masked, 'pcol', axis=1, tiled=True)  6.5 us
  transfers between devices with their start and end apart: 11, of which 10 were waited for; matrix products, arithmetic and copies ran while one was open for 1% of the time, Pallas kernels for 0%

profile of v1, /device:TPU:0, one launch (start us, length us, event | category | flops | bytes accessed | tf_op | source)
XLA Modules:
  0.0 223.7 jit_solution(4579817308020850942)
XLA Ops:
  7.2 0.7 convert_bitcast_fusion
  7.9 0.7 convolution_compare_fusion
  8.6 0.9 broadcast_select_fusion
  9.6 3.0 %collective-permute-start = (bf16[2,16,2048]{2,1,0:T(8,128)(2,1)S(1)}, bf16[2,16,2048]{2,1,0:T(8,128)(2,1)S(1)}, u32[]{:S(2)}, u32[]{:S(2)}) collective-permute-start(bf16[2,16,2048]{2,1,0:T(8,128)(2,1)S(1)} %broadcast_select_fusion), channel_id=1, source_target_pairs={{0,4},{4,8},{8,12},{12,16},{16,20},{20,24},{24,28},{28,0},{1,5},{5... | collective-permute-start | bytes 393224 | tf_op jit(solution)/shard_map/ppermute | solution.py:54
  12.6 6.5 %collective-permute-done = bf16[2,16,2048]{2,1,0:T(8,128)(2,1)S(1)} collective-permute-done((bf16[2,16,2048]{2,1,0:T(8,128)(2,1)S(1)}, bf16[2,16,2048]{2,1,0:T(8,128)(2,1)S(1)}, u32[]{:S(2)}, u32[]{:S(2)}) %collective-permute-start) | collective-permute-done | bytes 131104 | tf_op jit(solution)/shard_map/ppermute | solution.py:54
  19.2 7.7 %collective-permute-done.1 = bf16[2,16,2048]{2,1,0:T(8,128)(2,1)S(1)} collective-permute-done((bf16[2,16,2048]{2,1,0:T(8,128)(2,1)S(1)}, bf16[2,16,2048]{2,1,0:T(8,128)(2,1)S(1)}, u32[]{:S(2)}, u32[]{:S(2)}) %collective-permute-start.1) | collective-permute-done | bytes 131104 | tf_op jit(solution)/shard_map/ppermute | solution.py:54
  26.8 7.7 %collective-permute-done.2 = bf16[2,16,2048]{2,1,0:T(8,128)(2,1)S(1)} collective-permute-done((bf16[2,16,2048]{2,1,0:T(8,128)(2,1)S(1)}, bf16[2,16,2048]{2,1,0:T(8,128)(2,1)S(1)}, u32[]{:S(2)}, u32[]{:S(2)}) %collective-permute-start.2) | collective-permute-done | bytes 131104 | tf_op jit(solution)/shard_map/ppermute | solution.py:54
  34.5 7.7 %collective-permute-done.3 = bf16[2,16,2048]{2,1,0:T(8,128)(2,1)S(1)} collective-permute-done((bf16[2,16,2048]{2,1,0:T(8,128)(2,1)S(1)}, bf16[2,16,2048]{2,1,0:T(8,128)(2,1)S(1)}, u32[]{:S(2)}, u32[]{:S(2)}) %collective-permute-start.3) | collective-permute-done | bytes 131104 | tf_op jit(solution)/shard_map/ppermute | solution.py:54
  42.2 0.9 copy.9
  43.0 0.7 reshape.60
  43.8 3.3 %all-to-all-start = ((bf16[4,2,2048]{2,1,0:T(2,128)(2,1)}), bf16[4,2,2048]{2,1,0:T(2,128)(2,1)S(1)}, u32[]{:S(2)}, u32[]{:S(2)}) async-start(bf16[4,2,2048]{2,1,0:T(2,128)(2,1)} %reshape.60), calls=%async_computation | async-start | bytes 65536 | tf_op jit(solution)/shard_map/all_to_all | solution.py:49
  47.1 3.8 %all-to-all-done = bf16[4,2,2048]{2,1,0:T(2,128)(2,1)S(1)} async-done(((bf16[4,2,2048]{2,1,0:T(2,128)(2,1)}), bf16[4,2,2048]{2,1,0:T(2,128)(2,1)S(1)}, u32[]{:S(2)}, u32[]{:S(2)}) %all-to-all-start) | async-done | bytes 32800 | tf_op jit(solution)/shard_map/all_to_all | solution.py:49
  51.2 8.1 %collective-permute-done.5 = bf16[2,16,2048]{2,1,0:T(8,128)(2,1)S(1)} collective-permute-done((bf16[2,16,2048]{2,1,0:T(8,128)(2,1)S(1)}, bf16[2,16,2048]{2,1,0:T(8,128)(2,1)S(1)}, u32[]{:S(2)}, u32[]{:S(2)}) %collective-permute-start.5) | collective-permute-done | bytes 131104 | tf_op jit(solution)/shard_map/ppermute | solution.py:54
  59.3 7.7 %collective-permute-done.6 = bf16[2,16,2048]{2,1,0:T(8,128)(2,1)S(1)} collective-permute-done((bf16[2,16,2048]{2,1,0:T(8,128)(2,1)S(1)}, bf16[2,16,2048]{2,1,0:T(8,128)(2,1)S(1)}, u32[]{:S(2)}, u32[]{:S(2)}) %collective-permute-start.6) | collective-permute-done | bytes 131104 | tf_op jit(solution)/shard_map/ppermute | solution.py:54
  68.4 1.0 pad_maximum_fusion.1
  69.6 6.5 %all_gather.6 = bf16[2,64,2048]{2,1,0:T(8,128)(2,1)S(1)} all-gather(bf16[2,16,2048]{2,1,0:T(8,128)(2,1)S(1)} %broadcast_select_fusion), channel_id=1, replica_groups=mesh['prow'=8,'pcol'=4] {'pcol'}, dimensions={1}, use_global_device_ids=true | all-gather | bytes 655360 | tf_op jit(solution)/shard_map/all_gather | solution.py:46
  76.1 0.4 fusion.7
  76.4 13.8 %reduce-scatter.3.cloned.1.call-done = f32[2,64,512]{2,1,0:T(8,128)} async-done(((f32[2,64,2048]{2,1,0:T(8,128)}), f32[2,64,512]{2,1,0:T(8,128)}) %reduce-scatter.3.cloned.1.call-update) | async-done | bytes 262160 | tf_op jit(solution)/shard_map/reduce_scatter | solution.py:62
  90.2 1.6 fusion.31
  92.2 0.3 fusion.10
  93.2 1.5 pad_maximum_fusion
  94.8 68.7 %reduce-scatter.5.cloned.1.call-done = f32[2,64,512]{2,1,0:T(8,128)} async-done(((f32[2,512,512]{2,1,0:T(8,128)}), f32[2,64,512]{2,1,0:T(8,128)}) %reduce-scatter.5.cloned.1.call-update) | async-done | bytes 262160 | tf_op jit(solution)/shard_map/reduce_scatter | solution.py:74
  163.4 50.3 %all-gather.2.cloned.1.call-done = f32[2,512,512]{2,1,0:T(8,128)} async-done(((f32[2,64,512]{2,1,0:T(8,128)}), f32[2,512,512]{2,1,0:T(8,128)}) %all-gather.2.cloned.1.call-update) | async-done | bytes 2097168 | tf_op jit(solution)/shard_map/all_gather | solution.py:77
  213.8 3.4 %add.92 = f32[2,512,512]{2,1,0:T(8,128)} add(f32[2,512,512]{2,1,0:T(8,128)S(1)} %copy-done, f32[2,512,512]{2,1,0:T(8,128)} %all-gather.2.cloned.1.call-done) | non-fusion elementwise | flops 524288 | bytes 6291456 | tf_op jit(solution)/shard_map/add | solution.py:78
  (48 shorter events, 2.7 us)
Async XLA Ops:
  7.2 59.9 %copy-start.1 = (bf16[2,16,2048]{2,1,0:T(8,128)(2,1)S(1)}, bf16[2,16,2048]{2,1,0:T(8,128)(2,1)}, u32[]{:S(2)}) copy-start(bf16[2,16,2048]{2,1,0:T(8,128)(2,1)} %param.5) | copy-start | bytes 393220
  9.6 9.6 %collective-permute-start = (bf16[2,16,2048]{2,1,0:T(8,128)(2,1)S(1)}, bf16[2,16,2048]{2,1,0:T(8,128)(2,1)S(1)}, u32[]{:S(2)}, u32[]{:S(2)}) collective-permute-start(bf16[2,16,2048]{2,1,0:T(8,128)(2,1)S(1)} %broadcast_select_fusion), channel_id=1, source_target_pairs={{0,4},{4,8},{8,12},{12,16},{16,20},{20,24},{24,28},{28,0},{1,5},{5... | collective-permute-start | bytes 393224 | tf_op jit(solution)/shard_map/ppermute | solution.py:54
  19.2 7.7 %collective-permute-start.1 = (bf16[2,16,2048]{2,1,0:T(8,128)(2,1)S(1)}, bf16[2,16,2048]{2,1,0:T(8,128)(2,1)S(1)}, u32[]{:S(2)}, u32[]{:S(2)}) collective-permute-start(bf16[2,16,2048]{2,1,0:T(8,128)(2,1)S(1)} %collective-permute-done), channel_id=1, source_target_pairs={{0,4},{4,8},{8,12},{12,16},{16,20},{20,24},{24,28},{28,0},{1,5},{5... | collective-permute-start | bytes 393224 | tf_op jit(solution)/shard_map/ppermute | solution.py:54
  26.8 7.7 %collective-permute-start.2 = (bf16[2,16,2048]{2,1,0:T(8,128)(2,1)S(1)}, bf16[2,16,2048]{2,1,0:T(8,128)(2,1)S(1)}, u32[]{:S(2)}, u32[]{:S(2)}) collective-permute-start(bf16[2,16,2048]{2,1,0:T(8,128)(2,1)S(1)} %collective-permute-done.1), channel_id=1, source_target_pairs={{0,4},{4,8},{8,12},{12,16},{16,20},{20,24},{24,28},{28,0},{1,5},{5... | collective-permute-start | bytes 393224 | tf_op jit(solution)/shard_map/ppermute | solution.py:54
  34.5 7.7 %collective-permute-start.3 = (bf16[2,16,2048]{2,1,0:T(8,128)(2,1)S(1)}, bf16[2,16,2048]{2,1,0:T(8,128)(2,1)S(1)}, u32[]{:S(2)}, u32[]{:S(2)}) collective-permute-start(bf16[2,16,2048]{2,1,0:T(8,128)(2,1)S(1)} %collective-permute-done.2), channel_id=1, source_target_pairs={{0,4},{4,8},{8,12},{12,16},{16,20},{20,24},{24,28},{28,0},{1,5},{5... | collective-permute-start | bytes 393224 | tf_op jit(solution)/shard_map/ppermute | solution.py:54
  42.1 8.9 %collective-permute-start.4 = (bf16[2,16,2048]{2,1,0:T(8,128)(2,1)S(1)}, bf16[2,16,2048]{2,1,0:T(8,128)(2,1)S(1)}, u32[]{:S(2)}, u32[]{:S(2)}) collective-permute-start(bf16[2,16,2048]{2,1,0:T(8,128)(2,1)S(1)} %collective-permute-done.3), channel_id=1, source_target_pairs={{0,4},{4,8},{8,12},{12,16},{16,20},{20,24},{24,28},{28,0},{1,5},{5... | collective-permute-start | bytes 393224 | tf_op jit(solution)/shard_map/ppermute | solution.py:54
  43.8 7.2 %all-to-all-start = ((bf16[4,2,2048]{2,1,0:T(2,128)(2,1)}), bf16[4,2,2048]{2,1,0:T(2,128)(2,1)S(1)}, u32[]{:S(2)}, u32[]{:S(2)}) async-start(bf16[4,2,2048]{2,1,0:T(2,128)(2,1)} %reshape.60), calls=%async_computation | async-start | bytes 65536 | tf_op jit(solution)/shard_map/all_to_all | solution.py:49
  47.0 43.2 %reduce-scatter.3.cloned.1.call-start = ((), (), s32[]{:S(2)}) async-start(), calls=%async_computation.3 | async-start | bytes 1310720 | tf_op jit(solution)/shard_map/reduce_scatter | solution.py:62
  51.1 8.2 %collective-permute-start.5 = (bf16[2,16,2048]{2,1,0:T(8,128)(2,1)S(1)}, bf16[2,16,2048]{2,1,0:T(8,128)(2,1)S(1)}, u32[]{:S(2)}, u32[]{:S(2)}) collective-permute-start(bf16[2,16,2048]{2,1,0:T(8,128)(2,1)S(1)} %collective-permute-done.4), channel_id=1, source_target_pairs={{0,4},{4,8},{8,12},{12,16},{16,20},{20,24},{24,28},{28,0},{1,5},{5... | collective-permute-start | bytes 393224 | tf_op jit(solution)/shard_map/ppermute | solution.py:54
  59.2 7.7 %collective-permute-start.6 = (bf16[2,16,2048]{2,1,0:T(8,128)(2,1)S(1)}, bf16[2,16,2048]{2,1,0:T(8,128)(2,1)S(1)}, u32[]{:S(2)}, u32[]{:S(2)}) collective-permute-start(bf16[2,16,2048]{2,1,0:T(8,128)(2,1)S(1)} %collective-permute-done.5), channel_id=1, source_target_pairs={{0,4},{4,8},{8,12},{12,16},{16,20},{20,24},{24,28},{28,0},{1,5},{5... | collective-permute-start | bytes 393224 | tf_op jit(solution)/shard_map/ppermute | solution.py:54
  69.4 94.0 %reduce-scatter.5.cloned.1.call-start = ((), (), s32[]{:S(2)}) async-start(), calls=%async_computation.4 | async-start | bytes 2359296 | tf_op jit(solution)/shard_map/reduce_scatter | solution.py:74
  94.7 119.1 %copy-start = (f32[2,512,512]{2,1,0:T(8,128)S(1)}, f32[2,512,512]{2,1,0:T(8,128)}, u32[]{:S(2)}) copy-start(f32[2,512,512]{2,1,0:T(8,128)} %param.7) | copy-start | bytes 6291460
  94.7 119.0 %all-gather.2.cloned.1.call-start = ((), (), s32[]{:S(2)}) async-start(), calls=%async_computation.5 | async-start | bytes 2359296 | tf_op jit(solution)/shard_map/all_gather | solution.py:77
Sparse Core Ops, SparseCore 0:
  69.6 20.6 reduce-scatter.2
  94.8 68.5 reduce-scatter.4
  165.6 48.0 all-gather.1
